TPU v7x, 32 devices: a whole 2x2x4 slice. The times are simulated.
32 devices in a mesh: parts: 2 (over y), gz: 8 (over z, x), gy: 2 (over core).
Axes of the slice: x: 2, y: 2, z: 4, core: 2. Of those that a mesh axis runs over, the one named last changes fastest.
Arguments:
- direction: float32 [3, 16, 128, 128], P(None, ('parts', 'gz'), 'gy'), parts along dimension 1, may hold values from -6 to 6
- region: int32 [16, 128, 128], P(('parts', 'gz'), 'gy'), parts along dimension 0, may hold values from 0 to 3
- saturation: float32 [3], replicated, may hold values from 0.5 to 2
- kernel_main: float32 [6, 16, 256, 128], P(None, 'gz', 'gy'), may hold values from -6 to 6
- kernel_nyq: float32 [6, 16, 256], P(None, 'gz', 'gy'), may hold values from -6 to 6
Outputs:
- field: float32 [3, 16, 128, 128], P(None, ('parts', 'gz'), 'gy'), parts along dimension 1
There are 2 independent parts, one for each index of `parts`. A program takes and returns all parts, laid end to end along the dimension named above; an argument that names none is the same for every part. Nothing has to cross between parts.
Inputs may be any that keep to these rules, and one draw needn't show every extreme that they name: `region`: 0 marks an empty cell; other ids name materials.
All inputs are finite; a program needn't handle non-finite values.
Results may differ from a plain program's by a relative error of at most 0.00007.
Values sent between devices are 32-bit elements; how exact they have to be, the bound alone decides.
A program may use at most 64 MiB of HBM per device.

v0:
```python
import math

import jax
import jax.numpy as jnp
from jax import lax
from jax.sharding import PartitionSpec as P

exchange_stiffness = 0.25
tensor_index = ((0, 3, 4), (3, 1, 5), (4, 5, 2))
highest = lax.Precision.HIGHEST


def with_halo(cells, sides, width):
    for axis, dim in sides:
        count = lax.axis_size(axis)
        ends = count - 1
        head = lax.slice_in_dim(cells, 0, width, axis=dim)
        tail = lax.slice_in_dim(cells, cells.shape[dim] - width, cells.shape[dim], axis=dim)
        cells = jnp.concatenate(
            [
                lax.ppermute(tail, axis, [(i, (i + 1) % count) for i in range(ends)]),
                cells,
                lax.ppermute(head, axis, [((i + 1) % count, i) for i in range(ends)]),
            ],
            axis=dim,
        )
    return cells


def phase(first, second, period):
    product = first[:, None] * second[None, :] % period
    angle = 2.0 * math.pi / period * product.astype(jnp.float32)
    return (jnp.cos(angle), jnp.sin(angle))


def slot_frequency(slot_index, bit_count):
    device = slot_index // 2
    reversed_bits = jnp.zeros_like(device)
    for b in range(bit_count):
        reversed_bits = reversed_bits + device // 2**b % 2 * 2 ** (bit_count - 1 - b)
    return 2 * reversed_bits + slot_index % 2


def row_transform(plane):
    columns = plane.shape[2]
    row_count = plane.shape[1]
    positions = jnp.arange(columns, dtype=jnp.int32)
    cosine, sine = phase(positions, positions, 2 * columns)
    table = jnp.concatenate([cosine, -sine], axis=1)
    flat = plane.reshape(3 * row_count, columns)
    both = jnp.dot(flat, table, precision=highest).reshape(3, row_count, 2, columns)
    signs = 1.0 - 2.0 * (positions % 2).astype(jnp.float32)
    nyquist = jnp.dot(flat, signs, precision=highest).reshape(3, row_count)
    return (both[:, :, 0], both[:, :, 1], nyquist)


def column_transform(real_rows, imag_rows, nyquist, cosine, sine):
    new_real = jnp.einsum("kr,crx->ckx", cosine, real_rows, precision=highest) + jnp.einsum(
        "kr,crx->ckx", sine, imag_rows, precision=highest
    )
    new_imag = jnp.einsum("kr,crx->ckx", cosine, imag_rows, precision=highest) - jnp.einsum(
        "kr,crx->ckx", sine, real_rows, precision=highest
    )
    nyq_real = jnp.einsum("kr,cr->ck", cosine, nyquist, precision=highest)
    nyq_imag = -jnp.einsum("kr,cr->ck", sine, nyquist, precision=highest)
    return (jnp.stack([new_real, new_imag], axis=1), jnp.stack([nyq_real, nyq_imag], axis=1))


def plane_transform(values, cosine, sine, direction_sign):
    real_part = values[:, 0]
    imag_part = values[:, 1]
    new_real = jnp.einsum(
        "pz,cz...->cp...", cosine, real_part, precision=highest
    ) - direction_sign * jnp.einsum("pz,cz...->cp...", sine, imag_part, precision=highest)
    new_imag = jnp.einsum(
        "pz,cz...->cp...", cosine, imag_part, precision=highest
    ) + direction_sign * jnp.einsum("pz,cz...->cp...", sine, real_part, precision=highest)
    return jnp.stack([new_real, new_imag], axis=1)


def apply_kernel(spectra, kernel):
    pieces = []
    for i in range(3):
        summed = kernel[tensor_index[i][0]] * spectra[0]
        for j in (1, 2):
            summed = summed + kernel[tensor_index[i][j]] * spectra[j]
        pieces.append(summed)
    return jnp.stack(pieces)


def local(direction, region, saturation, kernel_main, kernel_nyq):
    columns = direction.shape[3]
    own_rows = direction.shape[2]
    groups_y = lax.axis_size("gy")
    groups_z = lax.axis_size("gz")
    bit_count = groups_z.bit_length() - 1
    rows_total = own_rows * groups_y
    period_y = 2 * rows_total
    period_z = 2 * groups_z
    period_x = 2 * columns
    spec_rows = period_y // groups_y
    y_index = lax.axis_index("gy")
    magnetic = (region > 0).astype(jnp.float32)
    strength = jnp.zeros(region.shape, jnp.float32)
    for r in range(saturation.shape[0]):
        strength = strength + jnp.where(region == r + 1, saturation[r], 0.0)
    magnet_plane = (direction * strength[None])[:, 0]
    gathered = lax.all_gather(magnet_plane, "gy", axis=1, tiled=True)
    frequency = y_index * spec_rows + jnp.arange(spec_rows, dtype=jnp.int32)
    cosine, sine = phase(frequency, jnp.arange(rows_total, dtype=jnp.int32), period_y)
    real_rows, imag_rows, nyquist = row_transform(gathered)
    spec_main, spec_nyq = column_transform(real_rows, imag_rows, nyquist, cosine, sine)
    slot_freq = slot_frequency(jnp.arange(period_z, dtype=jnp.int32), bit_count)
    plane_ids = jnp.arange(groups_z, dtype=jnp.int32)
    sent_main, sent_nyq = (
        lax.all_to_all(spec_main[:, :, None], "gz", split_axis=3, concat_axis=2, tiled=True),
        lax.all_to_all(spec_nyq[:, :, None], "gz", split_axis=3, concat_axis=2, tiled=True),
    )
    cosine, sine = phase(slot_freq, plane_ids, period_z)
    done_main = plane_transform(sent_main, cosine, sine, -1.0)
    done_nyq = plane_transform(sent_nyq, cosine, sine, -1.0)
    full_main, full_nyq = (
        lax.all_to_all(done_main, "gz", split_axis=2, concat_axis=3, tiled=True),
        lax.all_to_all(done_nyq, "gz", split_axis=2, concat_axis=3, tiled=True),
    )
    field_main = apply_kernel(full_main, kernel_main)
    field_nyq = apply_kernel(full_nyq, kernel_nyq)
    out_main, out_nyq = (
        lax.all_to_all(field_main, "gz", split_axis=3, concat_axis=2, tiled=True),
        lax.all_to_all(field_nyq, "gz", split_axis=3, concat_axis=2, tiled=True),
    )
    cosine, sine = phase(plane_ids, slot_freq, period_z)
    back_main = plane_transform(out_main, cosine, sine, 1.0)
    back_nyq = plane_transform(out_nyq, cosine, sine, 1.0)
    plane_main, plane_nyq = (
        lax.all_to_all(back_main, "gz", split_axis=2, concat_axis=3, tiled=True),
        lax.all_to_all(back_nyq, "gz", split_axis=2, concat_axis=3, tiled=True),
    )
    plane_main = plane_main[:, :, 0]
    plane_nyq = plane_nyq[:, :, 0]
    frequency = y_index * spec_rows + jnp.arange(spec_rows, dtype=jnp.int32)
    cosine, sine = phase(jnp.arange(rows_total, dtype=jnp.int32), frequency, period_y)
    term_real = jnp.einsum("yk,ckx->cyx", cosine, plane_main[:, 0], precision=highest) - jnp.einsum(
        "yk,ckx->cyx", sine, plane_main[:, 1], precision=highest
    )
    term_imag = jnp.einsum("yk,ckx->cyx", cosine, plane_main[:, 1], precision=highest) + jnp.einsum(
        "yk,ckx->cyx", sine, plane_main[:, 0], precision=highest
    )
    nyq_real = jnp.einsum("yk,ck->cy", cosine, plane_nyq[:, 0], precision=highest) - jnp.einsum(
        "yk,ck->cy", sine, plane_nyq[:, 1], precision=highest
    )
    nyq_imag = jnp.einsum("yk,ck->cy", cosine, plane_nyq[:, 1], precision=highest) + jnp.einsum(
        "yk,ck->cy", sine, plane_nyq[:, 0], precision=highest
    )
    rows_main, rows_nyq = (
        lax.psum_scatter(
            jnp.stack([term_real, term_imag], axis=1), "gy", scatter_dimension=2, tiled=True
        ),
        lax.psum_scatter(
            jnp.stack([nyq_real, nyq_imag], axis=1), "gy", scatter_dimension=2, tiled=True
        ),
    )
    positions = jnp.arange(columns, dtype=jnp.int32)
    cosine, sine = phase(positions, positions, period_x)
    weights = jnp.where(positions == 0, 1.0, 2.0).astype(jnp.float32)[:, None]
    table = jnp.concatenate([weights * cosine, -weights * sine], axis=0)
    flat = jnp.concatenate([rows_main[:, 0], rows_main[:, 1]], axis=2).reshape(
        3 * own_rows, 2 * columns
    )
    signs = 1.0 - 2.0 * (positions % 2).astype(jnp.float32)
    demag = jnp.dot(flat, table, precision=highest).reshape(3, own_rows, columns)
    demag = demag + rows_nyq[:, 0][:, :, None] * signs[None, None, :]
    demag = demag * (1.0 / (period_x * period_y * period_z))
    moment = direction * magnetic[None]
    stacked = jnp.concatenate([moment, magnetic[None]], axis=0)
    rim = with_halo(stacked, (("gz", 1), ("gy", 2)), 1)
    centre = rim[:, 1:2, 1:-1]
    near = rim[:, 0:1, 1:-1] + rim[:, 2:3, 1:-1] + rim[:, 1:2, :-2] + rim[:, 1:2, 2:]
    padded_x = jnp.pad(centre, ((0, 0), (0, 0), (0, 0), (1, 1)))
    near = near + padded_x[..., :-2] + padded_x[..., 2:]
    exchange = exchange_stiffness * magnetic[None] * (near[:3] - near[3:4] * direction)
    return demag[:, None] + exchange


def solution(mesh):
    placed = (
        P(None, ("parts", "gz"), "gy", None),
        P(("parts", "gz"), "gy", None),
        P(),
        P(None, "gz", "gy", None),
        P(None, "gz", "gy"),
    )
    return jax.shard_map(
        local,
        mesh=mesh,
        in_specs=placed,
        out_specs=P(None, ("parts", "gz"), "gy", None),
        check_vma=False,
    )
```

profile of v0, /device:TPU:0, one launch (start us, length us, event | category | flops | bytes accessed | tf_op | source)
XLA Modules:
  0.0 176.9 jit_solution(13148347249901439266)
XLA Ops:
  6.5 0.6 copy-done.4
  7.2 0.6 fusion.308
  7.8 0.8 broadcast_multiply_fusion.2
  8.7 0.7 copy-done.2
  9.4 1.9 %add_bitcast_fusion = f32[64,128]{1,0:T(8,128)S(1)} fusion(s32[1,64,128]{2,1,0:T(8,128)S(1)} %copy-done.2, f32[]{:T(128)} %bitcast.4, f32[]{:T(128)} %bitcast.3, f32[]{:T(128)} %bitcast.2), kind=kLoop, calls=%fused_computation.163 | loop fusion | flops 65536 | bytes 65548 | tf_op jit(solution)/shard_map/mul | solution.py:107
  11.3 2.1 %all-gather = f32[3,1,128,128]{3,2,0,1:T(8,128)S(1)} all-gather(f32[3,1,64,128]{3,2,0,1:T(8,128)S(1)} %get-tuple-element.28), channel_id=2, replica_groups=mesh['parts'=2,'gz'=8,'gy'=2] {'gy'}, dimensions={2}, use_global_device_ids=true | all-gather | bytes 294912 | tf_op jit(solution)/shard_map/all_gather | solution.py:108
  13.7 0.5 convolution_bitcast_fusion
  14.2 0.5 fusion.20
  14.8 0.8 copy.150
  15.6 7.1 %all-to-all-start.4 = ((f32[3,2,1,128]{0,1,2,3:T(2,128)}), f32[3,2,1,128]{0,1,2,3:T(2,128)S(1)}, u32[]{:S(2)}, u32[]{:S(2)}) async-start(f32[3,2,1,128]{0,1,2,3:T(2,128)} %copy.150), calls=%async_computation.4 | async-start | bytes 262144 | tf_op jit(solution)/shard_map/all_to_all | solution.py:117
  23.2 0.5 fusion.32
  23.6 0.7 fusion.36
  24.3 0.7 fusion.37
  25.0 0.7 fusion.7
  25.7 0.7 fusion.6
  26.4 3.7 %all-to-all-done.4 = f32[3,2,1,128]{0,1,2,3:T(2,128)S(1)} async-done(((f32[3,2,1,128]{0,1,2,3:T(2,128)}), f32[3,2,1,128]{0,1,2,3:T(2,128)S(1)}, u32[]{:S(2)}, u32[]{:S(2)}) %all-to-all-start.4) | async-done | bytes 3104 | tf_op jit(solution)/shard_map/all_to_all | solution.py:117
  31.5 0.7 reshape.497
  32.2 3.3 %all-to-all-start.5 = ((f32[8,1,192]{2,1,0:T(1,128)}), f32[8,1,192]{2,1,0:T(1,128)S(1)}, u32[]{:S(2)}, u32[]{:S(2)}) async-start(f32[8,1,192]{2,1,0:T(1,128)} %reshape.497), calls=%async_computation.5 | async-start | bytes 16384 | tf_op jit(solution)/shard_map/all_to_all | solution.py:124
  35.6 0.9 copy.131
  36.5 5.5 %all-to-all-done.5 = f32[8,1,192]{2,1,0:T(1,128)S(1)} async-done(((f32[8,1,192]{2,1,0:T(1,128)}), f32[8,1,192]{2,1,0:T(1,128)S(1)}, u32[]{:S(2)}, u32[]{:S(2)}) %all-to-all-start.5) | async-done | bytes 6176 | tf_op jit(solution)/shard_map/all_to_all | solution.py:124
  42.0 3.5 %all-to-all-start = ((f32[3,2,1,128,128]{4,1,2,0,3:T(2,128)}), f32[3,2,1,128,128]{4,1,2,0,3:T(2,128)S(1)}, u32[]{:S(2)}, u32[]{:S(2)}) async-start(f32[3,2,1,128,128]{4,1,2,0,3:T(2,128)} %copy.131), calls=%async_computation | async-start | bytes 786432 | tf_op jit(solution)/shard_map/all_to_all | solution.py:116
  45.5 0.5 broadcast.794
  46.0 0.6 reduce
  47.2 1.0 reshape.499
  48.2 7.0 %all-to-all-done = f32[3,2,1,128,128]{4,1,2,0,3:T(2,128)S(1)} async-done(((f32[3,2,1,128,128]{4,1,2,0,3:T(2,128)}), f32[3,2,1,128,128]{4,1,2,0,3:T(2,128)S(1)}, u32[]{:S(2)}, u32[]{:S(2)}) %all-to-all-start) | async-done | bytes 393248 | tf_op jit(solution)/shard_map/all_to_all | solution.py:116
  55.2 3.7 %all-to-all-start.6 = ((f32[8,1,192]{2,1,0:T(1,128)}), f32[8,1,192]{2,1,0:T(1,128)S(1)}, u32[]{:S(2)}, u32[]{:S(2)}) async-start(f32[8,1,192]{2,1,0:T(1,128)} %reshape.499), calls=%async_computation.6 | async-start | bytes 16384 | tf_op jit(solution)/shard_map/all_to_all | solution.py:130
  58.9 0.6 convolution_multiply_fusion.1
  59.5 0.6 convolution_multiply_fusion
  60.1 0.6 fusion.1
  60.7 0.6 fusion
  61.3 1.1 copy.135
  62.4 2.9 %all-to-all-done.6 = f32[8,1,192]{2,1,0:T(1,128)S(1)} async-done(((f32[8,1,192]{2,1,0:T(1,128)}), f32[8,1,192]{2,1,0:T(1,128)S(1)}, u32[]{:S(2)}, u32[]{:S(2)}) %all-to-all-start.6) | async-done | bytes 6176 | tf_op jit(solution)/shard_map/all_to_all | solution.py:130
  65.4 3.5 %all-to-all-start.1 = ((f32[3,2,16,16,128]{4,3,0,1,2:T(8,128)}), f32[3,2,16,16,128]{4,3,0,1,2:T(8,128)S(1)}, u32[]{:S(2)}, u32[]{:S(2)}) async-start(f32[3,2,16,16,128]{4,3,0,1,2:T(8,128)} %copy.135), calls=%async_computation.1 | async-start | bytes 1572864 | tf_op jit(solution)/shard_map/all_to_all | solution.py:123
  69.0 0.6 reduce.1
  71.1 0.6 copy.162
  71.7 15.7 %all-to-all-done.1 = f32[3,2,16,16,128]{4,3,0,1,2:T(8,128)S(1)} async-done(((f32[3,2,16,16,128]{4,3,0,1,2:T(8,128)}), f32[3,2,16,16,128]{4,3,0,1,2:T(8,128)S(1)}, u32[]{:S(2)}, u32[]{:S(2)}) %all-to-all-start.1) | async-done | bytes 786464 | tf_op jit(solution)/shard_map/all_to_all | solution.py:123
  87.4 3.5 %all-to-all-start.7 = ((f32[3,2,8,16]{3,1,0,2:T(2,128)}), f32[3,2,8,16]{3,1,0,2:T(2,128)S(1)}, u32[]{:S(2)}, u32[]{:S(2)}) async-start(f32[3,2,8,16]{3,1,0,2:T(2,128)} %copy.162), calls=%async_computation.7 | async-start | bytes 49152 | tf_op jit(solution)/shard_map/all_to_all | solution.py:137
  91.4 1.5 copy.140
  92.9 4.7 %all-to-all-done.7 = f32[3,2,8,16]{3,1,0,2:T(2,128)S(1)} async-done(((f32[3,2,8,16]{3,1,0,2:T(2,128)}), f32[3,2,8,16]{3,1,0,2:T(2,128)S(1)}, u32[]{:S(2)}, u32[]{:S(2)}) %all-to-all-start.7) | async-done | bytes 3104 | tf_op jit(solution)/shard_map/all_to_all | solution.py:137
  97.6 3.5 %all-to-all-start.2 = ((f32[3,2,2,128,128]{4,2,1,0,3:T(2,128)}), f32[3,2,2,128,128]{4,2,1,0,3:T(2,128)S(1)}, u32[]{:S(2)}, u32[]{:S(2)}) async-start(f32[3,2,2,128,128]{4,2,1,0,3:T(2,128)} %copy.140), calls=%async_computation.2 | async-start | bytes 1572864 | tf_op jit(solution)/shard_map/all_to_all | solution.py:129
  101.1 3.8 %collective-permute-start = (f32[4,1,64,128]{3,2,0,1:T(8,128)S(1)}, f32[4,1,64,128]{3,2,0,1:T(8,128)S(1)}, u32[]{:S(2)}, u32[]{:S(2)}) collective-permute-start(f32[4,1,64,128]{3,2,0,1:T(8,128)S(1)} %pad_maximum_fusion.12), channel_id=1, source_target_pairs={{0,2},{2,4},{4,6},{6,8},{8,10},{10,12},{12,14},{1,3},{3,5},{5,7},{... | collective-permute-start | bytes 393224 | tf_op jit(solution)/shard_map/ppermute | solution.py:21
  105.0 1.5 collective-permute-start.1
  107.3 13.6 %all-to-all-done.2 = f32[3,2,2,128,128]{4,2,1,0,3:T(2,128)S(1)} async-done(((f32[3,2,2,128,128]{4,2,1,0,3:T(2,128)}), f32[3,2,2,128,128]{4,2,1,0,3:T(2,128)S(1)}, u32[]{:S(2)}, u32[]{:S(2)}) %all-to-all-start.2) | async-done | bytes 786464 | tf_op jit(solution)/shard_map/all_to_all | solution.py:129
  120.9 0.6 copy.142
  123.0 0.8 copy.143
  123.9 3.5 %all-to-all-start.3 = ((f32[3,2,8,16,128]{4,3,0,1,2:T(8,128)}), f32[3,2,8,16,128]{4,3,0,1,2:T(8,128)S(1)}, u32[]{:S(2)}, u32[]{:S(2)}) async-start(f32[3,2,8,16,128]{4,3,0,1,2:T(8,128)} %copy.143), calls=%async_computation.3 | async-start | bytes 786432 | tf_op jit(solution)/shard_map/all_to_all | solution.py:136
  127.4 0.4 fusion.19
  127.8 0.5 fusion.81
  128.2 0.5 fusion.18
  128.9 0.8 reshape.494
  129.8 0.6 copy-done.5
  130.4 0.7 dynamic-slice
  131.8 7.5 %reduce-scatter.4.cloned.1.call-done = f32[64,6]{1,0:T(8,128)} async-done(((f32[128,6]{1,0:T(8,128)}), f32[64,6]{1,0:T(8,128)}) %reduce-scatter.4.cloned.1.call-update) | async-done | bytes 1552
  139.2 0.9 reshape.495
  140.2 2.1 %collective-permute-start.2 = (f32[4,3,1,128]{3,2,0,1:T(1,128)S(1)}, f32[4,3,1,128]{3,2,0,1:T(1,128)S(1)}, u32[]{:S(2)}, u32[]{:S(2)}) collective-permute-start(f32[4,3,1,128]{3,2,0,1:T(1,128)S(1)} %get-tuple-element.19), channel_id=1, source_target_pairs={{0,1},{2,3},{4,5},{6,7},{8,9},{10,11},{12,13},{14,15},{16,17},{18,... | collective-permute-start | bytes 18440 | tf_op jit(solution)/shard_map/ppermute | solution.py:21
  142.3 1.3 collective-permute-start.3
  143.7 0.6 fusion.38
  144.3 0.6 fusion.39
  145.0 0.6 fusion.3
  145.7 0.6 fusion.2
  146.3 0.9 copy.147
  147.5 20.4 %all-reduce.4.cloned.1.call-done = f32[3,2,128,128]{3,1,0,2:T(2,128)} async-done(((f32[3,2,128,128]{3,1,0,2:T(2,128)}), f32[3,2,128,128]{3,1,0,2:T(2,128)}) %all-reduce.4.cloned.1.call-update) | async-done | bytes 393232
  167.9 1.2 constant_dynamic-slice_fusion
  169.1 1.0 fusion.11
  (95 shorter events, 7.8 us)
Async XLA Ops:
  6.5 0.7 copy-start.4
  7.8 3.5 %copy-start.1 = (f32[3,1,64,128]{3,2,1,0:T(8,128)S(1)}, f32[3,1,64,128]{3,2,1,0:T(8,128)}, u32[]{:S(2)}) copy-start(f32[3,1,64,128]{3,2,1,0:T(8,128)} %param.5) | copy-start | bytes 294916
  8.6 0.8 copy-start.2
  15.6 14.5 %all-to-all-start.4 = ((f32[3,2,1,128]{0,1,2,3:T(2,128)}), f32[3,2,1,128]{0,1,2,3:T(2,128)S(1)}, u32[]{:S(2)}, u32[]{:S(2)}) async-start(f32[3,2,1,128]{0,1,2,3:T(2,128)} %copy.150), calls=%async_computation.4 | async-start | bytes 262144 | tf_op jit(solution)/shard_map/all_to_all | solution.py:117
  32.2 9.8 %all-to-all-start.5 = ((f32[8,1,192]{2,1,0:T(1,128)}), f32[8,1,192]{2,1,0:T(1,128)S(1)}, u32[]{:S(2)}, u32[]{:S(2)}) async-start(f32[8,1,192]{2,1,0:T(1,128)} %reshape.497), calls=%async_computation.5 | async-start | bytes 16384 | tf_op jit(solution)/shard_map/all_to_all | solution.py:124
  36.5 9.0 %copy-start.3 = (f32[6,2,128]{2,1,0:T(2,128)S(1)}, f32[6,2,128]{2,1,0:T(2,128)}, u32[]{:S(2)}) copy-start(f32[6,2,128]{2,1,0:T(2,128)} %param.9) | copy-start | bytes 18436
  42.0 13.2 %all-to-all-start = ((f32[3,2,1,128,128]{4,1,2,0,3:T(2,128)}), f32[3,2,1,128,128]{4,1,2,0,3:T(2,128)S(1)}, u32[]{:S(2)}, u32[]{:S(2)}) async-start(f32[3,2,1,128,128]{4,1,2,0,3:T(2,128)} %copy.131), calls=%async_computation | async-start | bytes 786432 | tf_op jit(solution)/shard_map/all_to_all | solution.py:116
  55.2 10.2 %all-to-all-start.6 = ((f32[8,1,192]{2,1,0:T(1,128)}), f32[8,1,192]{2,1,0:T(1,128)S(1)}, u32[]{:S(2)}, u32[]{:S(2)}) async-start(f32[8,1,192]{2,1,0:T(1,128)} %reshape.499), calls=%async_computation.6 | async-start | bytes 16384 | tf_op jit(solution)/shard_map/all_to_all | solution.py:130
  62.4 6.5 %copy-start = (f32[6,2,128,128]{3,2,1,0:T(8,128)S(1)}, f32[6,2,128,128]{3,2,1,0:T(8,128)}, u32[]{:S(2)}) copy-start(f32[6,2,128,128]{3,2,1,0:T(8,128)} %param.8) | copy-start | bytes 2359300
  65.4 22.0 %all-to-all-start.1 = ((f32[3,2,16,16,128]{4,3,0,1,2:T(8,128)}), f32[3,2,16,16,128]{4,3,0,1,2:T(8,128)S(1)}, u32[]{:S(2)}, u32[]{:S(2)}) async-start(f32[3,2,16,16,128]{4,3,0,1,2:T(8,128)} %copy.135), calls=%async_computation.1 | async-start | bytes 1572864 | tf_op jit(solution)/shard_map/all_to_all | solution.py:123
  87.4 10.2 %all-to-all-start.7 = ((f32[3,2,8,16]{3,1,0,2:T(2,128)}), f32[3,2,8,16]{3,1,0,2:T(2,128)S(1)}, u32[]{:S(2)}, u32[]{:S(2)}) async-start(f32[3,2,8,16]{3,1,0,2:T(2,128)} %copy.162), calls=%async_computation.7 | async-start | bytes 49152 | tf_op jit(solution)/shard_map/all_to_all | solution.py:137
  97.6 23.3 %all-to-all-start.2 = ((f32[3,2,2,128,128]{4,2,1,0,3:T(2,128)}), f32[3,2,2,128,128]{4,2,1,0,3:T(2,128)S(1)}, u32[]{:S(2)}, u32[]{:S(2)}) async-start(f32[3,2,2,128,128]{4,2,1,0,3:T(2,128)} %copy.140), calls=%async_computation.2 | async-start | bytes 1572864 | tf_op jit(solution)/shard_map/all_to_all | solution.py:129
  101.1 39.1 %collective-permute-start = (f32[4,1,64,128]{3,2,0,1:T(8,128)S(1)}, f32[4,1,64,128]{3,2,0,1:T(8,128)S(1)}, u32[]{:S(2)}, u32[]{:S(2)}) collective-permute-start(f32[4,1,64,128]{3,2,0,1:T(8,128)S(1)} %pad_maximum_fusion.12), channel_id=1, source_target_pairs={{0,2},{2,4},{4,6},{6,8},{8,10},{10,12},{12,14},{1,3},{3,5},{5,7},{... | collective-permute-start | bytes 393224 | tf_op jit(solution)/shard_map/ppermute | solution.py:21
  105.0 35.2 %collective-permute-start.1 = (f32[4,1,64,128]{3,2,0,1:T(8,128)S(1)}, f32[4,1,64,128]{3,2,0,1:T(8,128)S(1)}, u32[]{:S(2)}, u32[]{:S(2)}) collective-permute-start(f32[4,1,64,128]{3,2,0,1:T(8,128)S(1)} %pad_maximum_fusion.12), channel_id=1, source_target_pairs={{2,0},{4,2},{6,4},{8,6},{10,8},{12,10},{14,12},{3,1},{5,3},{7,5},{... | collective-permute-start | bytes 393224 | tf_op jit(solution)/shard_map/ppermute | solution.py:23
  123.9 19.8 %all-to-all-start.3 = ((f32[3,2,8,16,128]{4,3,0,1,2:T(8,128)}), f32[3,2,8,16,128]{4,3,0,1,2:T(8,128)S(1)}, u32[]{:S(2)}, u32[]{:S(2)}) async-start(f32[3,2,8,16,128]{4,3,0,1,2:T(8,128)} %copy.143), calls=%async_computation.3 | async-start | bytes 786432 | tf_op jit(solution)/shard_map/all_to_all | solution.py:136
  127.3 11.9 %reduce-scatter.4.cloned.1.call-start = ((), (), s32[]{:S(2)}) async-start(), calls=%async_computation.9 | async-start | bytes 98304
  129.7 38.2 %all-reduce.4.cloned.1.call-start = ((), (), s32[]{:S(2)}) async-start(), calls=%async_computation.10 | async-start | bytes 786432
  129.8 0.7 copy-start.5
  140.2 7.1 %collective-permute-start.2 = (f32[4,3,1,128]{3,2,0,1:T(1,128)S(1)}, f32[4,3,1,128]{3,2,0,1:T(1,128)S(1)}, u32[]{:S(2)}, u32[]{:S(2)}) collective-permute-start(f32[4,3,1,128]{3,2,0,1:T(1,128)S(1)} %get-tuple-element.19), channel_id=1, source_target_pairs={{0,1},{2,3},{4,5},{6,7},{8,9},{10,11},{12,13},{14,15},{16,17},{18,... | collective-permute-start | bytes 18440 | tf_op jit(solution)/shard_map/ppermute | solution.py:21
  142.3 4.9 %collective-permute-start.3 = (f32[4,3,1,128]{3,2,0,1:T(1,128)S(1)}, f32[4,3,1,128]{3,2,0,1:T(1,128)S(1)}, u32[]{:S(2)}, u32[]{:S(2)}) collective-permute-start(f32[4,3,1,128]{3,2,0,1:T(1,128)S(1)} %get-tuple-element.20), channel_id=1, source_target_pairs={{1,0},{3,2},{5,4},{7,6},{9,8},{11,10},{13,12},{15,14},{17,16},{19,... | collective-permute-start | bytes 18440 | tf_op jit(solution)/shard_map/ppermute | solution.py:23
Sparse Core Ops, SparseCore 0:
  130.3 8.8 reduce-scatter.3
  147.4 20.4 all-reduce.3
where the time goes:
time: 178 us; the launch traced here: 177 us
  waiting for transfers between devices  81 us (46%)
  starting transfers between devices  40.5 us (23%)
  local copies, waits for them, and re-layouts  18.3 us (10%)
  matrix products  15.2 us (9%)
  between operations  14.8 us (8%)
  other arithmetic  5.07 us (3%)
  blocking collectives  2.08 us (1%)
    unnamed x4, waiting for transfers between devices  27.9 us
    all_to_all x1, waiting for transfers between devices, local(): lax.all_to_all(done_main, 'gz', split_axis=2, concat_axis=3, tiled=True)  15.7 us
    all_to_all x1, waiting for transfers between devices, local(): lax.all_to_all(field_main, 'gz', split_axis=3, concat_axis=2, tiled=True)  13.6 us
    all_to_all x1, starting transfers between devices, local(): lax.all_to_all(spec_nyq[:, :, None], 'gz', split_axis=3, concat_axis=2, t...  7.15 us
    all_to_all x1, waiting for transfers between devices, local(): lax.all_to_all(spec_main[:, :, None], 'gz', split_axis=3, concat_axis=2,...  7.02 us
    unnamed x25, local copies, waits for them, and re-layouts  6.98 us
    ppermute x2, starting transfers between devices, with_halo(): lax.ppermute(tail, axis, [(i, (i + 1) % count) for i in range(ends)])  5.94 us
    all_to_all x1, waiting for transfers between devices, local(): lax.all_to_all(done_nyq, 'gz', split_axis=2, concat_axis=3, tiled=True)  5.5 us
  transfers between devices with their start and end apart: 14, of which 9 were waited for; matrix products, arithmetic and copies ran while one was open for 15% of the time, Pallas kernels for 0%

commit v1 on v0

--- a/solution.py
+++ b/solution.py
@@ -1,8 +1,12 @@
+import functools
 import math
 
 import jax
 import jax.numpy as jnp
+import numpy as np
 from jax import lax
+from jax.experimental import pallas as pl
+from jax.experimental.pallas import tpu as pltpu
 from jax.sharding import PartitionSpec as P
 
 exchange_stiffness = 0.25
@@ -182,6 +186,577 @@
     return demag[:, None] + exchange
 
 
+MESH = pl.DeviceIdType.MESH
+most_unrolled_planes = 16
+
+
+def halves(table):
+    high = table.astype(np.float32).astype(jnp.bfloat16)
+    low = (table - high.astype(np.float64)).astype(np.float32).astype(jnp.bfloat16)
+    return np.stack([high, low])
+
+
+@functools.lru_cache(maxsize=None)
+def tables(columns, rows_total, groups_y, groups_z):
+    x = np.arange(columns)
+    ang = np.pi / columns * (np.outer(x, x) % (2 * columns))
+    c, s = np.cos(ang), np.sin(ang)
+    fwd = np.block([[c, -s], [s, c]])
+    w = np.where(x == 0, 1.0, 2.0)[:, None]
+    inv = np.block([[w * c, w * s], [-w * s, w * c]])
+    tx = np.stack([halves(fwd), halves(inv)])
+    spec = 2 * rows_total // groups_y
+    y = np.arange(rows_total)
+    ty = []
+    for g in range(groups_y):
+        ky = g * spec + np.arange(spec)
+        ang = np.pi / rows_total * (np.outer(ky, y) % (2 * rows_total))
+        c, s = np.cos(ang), np.sin(ang)
+        f = np.block([[c, s], [-s, c]])
+        ty.append(np.stack([halves(f), halves(f.T)]))
+    ty = np.stack(ty)
+    signs = 1.0 - 2.0 * (x % 2)
+    gather = np.zeros((6 * columns, columns))
+    spread = np.zeros((columns, 6 * columns))
+    for b in range(6):
+        gather[b * columns : (b + 1) * columns, b] = signs
+        gather[b * columns : (b + 1) * columns, b + 6] = signs
+        spread[b, b * columns : (b + 1) * columns] = signs
+    pick = np.zeros((3, 12, columns))
+    for d in range(3):
+        for i in range(3):
+            for k in range(2):
+                pick[d, tensor_index[i][(i + d) % 3] * 2 + k, i * 2 + k] = 1.0
+    bits = groups_z.bit_length() - 1
+    coef = np.zeros((groups_z, 4 * groups_z))
+    plane = np.arange(groups_z)
+    for g in range(groups_z):
+        rev = sum(((g >> b) & 1) << (bits - 1 - b) for b in range(bits))
+        for k in range(2):
+            ang = np.pi / groups_z * ((2 * rev + k) * plane % (2 * groups_z))
+            coef[g, 2 * k :: 4] = np.cos(ang)
+            coef[g, 2 * k + 1 :: 4] = -np.sin(ang)
+    return (
+        tx,
+        ty,
+        gather.astype(jnp.bfloat16),
+        spread.astype(jnp.bfloat16),
+        pick.astype(np.float32),
+        coef.astype(np.float32),
+    )
+
+
+def split(value):
+    high = value.astype(jnp.bfloat16)
+    return high, (value - high.astype(jnp.float32)).astype(jnp.bfloat16)
+
+
+def mm(a, b):
+    return jnp.dot(a, b, preferred_element_type=jnp.float32)
+
+
+def fused(
+    coef,
+    sat,
+    direction,
+    region,
+    pick,
+    knyq,
+    kmain_hbm,
+    tx_hbm,
+    ty_hbm,
+    gather_hbm,
+    spread_hbm,
+    out,
+    mom,
+    strength,
+    near_strength,
+    exch,
+    kmain,
+    tx,
+    ty,
+    gather,
+    spread,
+    zh,
+    zl,
+    rh,
+    rl,
+    gh,
+    gl,
+    afull,
+    apeer,
+    xsend,
+    xrecv,
+    upsend,
+    uprecv,
+    dnsend,
+    dnrecv,
+    local_sem,
+    ag_send,
+    ag_ici,
+    ag_d2d,
+    s_send,
+    s_recv,
+    a_send,
+    a_recv,
+    x_ssem,
+    x_rsem,
+    up_ssem,
+    up_rsem,
+    dn_ssem,
+    dn_rsem,
+):
+    planes = mom.shape[0]
+    line = planes // 2
+    rows_total = mom.shape[2]
+    columns = mom.shape[3]
+    rows = direction.shape[2]
+    g = lax.axis_index("gz")
+    c = lax.axis_index("gy")
+    o = g // 2
+    xi = g % 2
+    side = g + 1 - 2 * xi
+    own = pl.ds(pl.multiple_of(c * rows, rows), rows)
+    other = pl.ds(pl.multiple_of((1 - c) * rows, rows), rows)
+    peer_id = {"gz": g, "gy": 1 - c}
+    side_id = {"gz": side, "gy": c}
+    up_id = {"gz": g + 2, "gy": c}
+    dn_id = {"gz": g - 2, "gy": c}
+    after_id = {"gz": g + 1, "gy": c}
+    before_id = {"gz": g - 1, "gy": c}
+    has_up = o < line - 1
+    has_dn = o > 0
+    has_after = g < planes - 1
+    has_before = g > 0
+
+    barrier = pltpu.get_barrier_semaphore()
+    pl.semaphore_signal(barrier, inc=1, device_id=peer_id, device_id_type=MESH)
+    pl.semaphore_signal(barrier, inc=1, device_id=side_id, device_id_type=MESH)
+    for cond, where in ((has_up, up_id), (has_dn, dn_id), (has_after, after_id), (has_before, before_id)):
+
+        @pl.when(cond)
+        def _(where=where):
+            pl.semaphore_signal(barrier, inc=1, device_id=where, device_id_type=MESH)
+
+    loads = [
+        pltpu.make_async_copy(kmain_hbm, kmain, local_sem.at[0]),
+        pltpu.make_async_copy(tx_hbm, tx, local_sem.at[1]),
+        pltpu.make_async_copy(ty_hbm.at[c], ty, local_sem.at[2]),
+        pltpu.make_async_copy(gather_hbm, gather, local_sem.at[3]),
+        pltpu.make_async_copy(spread_hbm, spread, local_sem.at[4]),
+    ]
+    for copy in loads:
+        copy.start()
+
+    reg = region[0]
+    s = jnp.zeros(reg.shape, jnp.float32)
+    for r in range(sat.shape[0]):
+        s = s + jnp.where(reg == r + 1, sat[r], 0.0)
+    strength[own, :] = s
+    for j in range(3):
+        mom[g, j, own, :] = direction[j, 0] * s
+
+    friends = 2
+    for cond in (has_up, has_dn, has_after, has_before):
+        friends = friends + jnp.where(cond, 1, 0)
+    pl.semaphore_wait(barrier, friends)
+
+    def chunk_copy(p, j, way):
+        where, recv = ((up_id, ag_ici), (dn_id, ag_ici), (side_id, ag_ici), (peer_id, ag_d2d))[way]
+        block = mom.at[p, j, own, :]
+        return pltpu.make_async_remote_copy(
+            src_ref=block,
+            dst_ref=block,
+            send_sem=ag_send.at[way, p, j],
+            recv_sem=recv.at[p, j],
+            device_id=where,
+            device_id_type=MESH,
+        )
+
+    def peer_arrival(p, j):
+        block = mom.at[p, j, other, :]
+        return pltpu.make_async_remote_copy(
+            src_ref=block,
+            dst_ref=block,
+            send_sem=ag_send.at[3, p, j],
+            recv_sem=ag_d2d.at[p, j],
+            device_id=peer_id,
+            device_id_type=MESH,
+        )
+
+    def when(cond, action):
+        pl.when(cond)(action)
+
+    for j in range(3):
+        when(has_up, lambda: chunk_copy(g, j, 0).start())
+        when(has_dn, lambda: chunk_copy(g, j, 1).start())
+        chunk_copy(g, j, 2).start()
+
+    def strength_copy(way):
+        where = (peer_id, after_id, before_id)[way]
+        if way == 0:
+            dst = strength.at[own, :]
+        else:
+            dst = near_strength.at[way - 1]
+        return pltpu.make_async_remote_copy(
+            src_ref=strength.at[own, :],
+            dst_ref=dst,
+            send_sem=s_send.at[way],
+            recv_sem=s_recv.at[way],
+            device_id=where,
+            device_id_type=MESH,
+        )
+
+    strength_copy(0).start()
+    when(has_after, lambda: strength_copy(1).start())
+    when(has_before, lambda: strength_copy(2).start())
+    for j in range(3):
+        chunk_copy(g, j, 3).start()
+
+    for h in range(1, line + 1):
+        for j in range(3):
+            if h < line:
+
+                @pl.when(o >= h)
+                def _():
+                    p = g - 2 * h
+                    chunk_copy(p, j, 2).wait_recv()
+                    when(has_up, lambda: chunk_copy(p, j, 0).start())
+                    chunk_copy(p, j, 2).start()
+                    chunk_copy(p, j, 3).start()
+
+                @pl.when(o + h < line)
+                def _():
+                    p = g + 2 * h
+                    chunk_copy(p, j, 2).wait_recv()
+                    when(has_dn, lambda: chunk_copy(p, j, 1).start())
+                    chunk_copy(p, j, 2).start()
+                    chunk_copy(p, j, 3).start()
+
+            def side_arrived(p):
+                chunk_copy(p, j, 2).wait_recv()
+                chunk_copy(p, j, 3).start()
+
+            if h == 1:
+                side_arrived(side)
+            else:
+                when(o >= h - 1, lambda: side_arrived(side - 2 * (h - 1)))
+                when(o + h - 1 < line, lambda: side_arrived(side + 2 * (h - 1)))
+
+    for copy in loads:
+        copy.wait()
+    for p in range(planes):
+        for j in range(3):
+            peer_arrival(p, j).wait_recv()
+
+    step = 32
+    for j in range(3):
+        for top in range(0, rows_total, step):
+            accs = [None] * 4
+            for p in range(planes):
+                m = mom[p, j, top : top + step, :]
+                for q in range(4):
+                    term = m * coef[g, 4 * p + q]
+                    accs[q] = term if accs[q] is None else accs[q] + term
+            for q in range(4):
+                hi, lo = split(accs[q])
+                at = (2 * j + q // 2) * rows_total + top
+                lanes = slice((q % 2) * columns, (q % 2 + 1) * columns)
+                zh[at : at + step, lanes] = hi
+                zl[at : at + step, lanes] = lo
+
+    nyq = [None, None]
+    for b in range(6):
+        band = slice(b * rows_total, (b + 1) * rows_total)
+        hi, lo = zh[band, :], zl[band, :]
+        res = mm(hi, tx[0, 0]) + mm(hi, tx[0, 1]) + mm(lo, tx[0, 0])
+        signs = gather[b * columns : (b + 1) * columns, :]
+        for q in range(2):
+            lanes = slice(q * columns, (q + 1) * columns)
+            band_out = slice(q * rows_total, (q + 1) * rows_total)
+            cols = slice(b * columns, (b + 1) * columns)
+            rhi, rlo = split(res[:, lanes])
+            rh[band_out, cols] = rhi
+            rl[band_out, cols] = rlo
+            n = mm(hi[:, lanes], signs) + mm(lo[:, lanes], signs)
+            nyq[q] = n if nyq[q] is None else nyq[q] + n
+    nyq_cols = slice(6 * columns, 7 * columns)
+    for q in range(2):
+        band_out = slice(q * rows_total, (q + 1) * rows_total)
+        rhi, rlo = split(nyq[q])
+        rh[band_out, nyq_cols] = rhi
+        rl[band_out, nyq_cols] = rlo
+
+    spec = kmain.shape[2]
+
+    def column_pass(t, b):
+        cols = slice(b * columns, (b + 1) * columns)
+        hi, lo = (rh, rl) if t == 0 else (gh, gl)
+        hi, lo = hi[:, cols], lo[:, cols]
+        return mm(ty[t, 0], hi) + mm(ty[t, 1], hi) + mm(ty[t, 0], lo)
+
+    for k in range(2):
+        spectra = [column_pass(0, 2 * j + k) for j in range(3)]
+        for i in range(3):
+            cols = slice((2 * i + k) * columns, (2 * i + k + 1) * columns)
+            for q in range(2):
+                band = slice(q * spec, (q + 1) * spec)
+                total = kmain[tensor_index[i][0], k] * spectra[0][band]
+                for j in (1, 2):
+                    total = total + kmain[tensor_index[i][j], k] * spectra[j][band]
+                hi, lo = split(total)
+                gh[band, cols] = hi
+                gl[band, cols] = lo
+    spectrum = column_pass(0, 6)
+    factors = knyq[...].reshape(12, spec)
+    totals = [None, None]
+    for d in range(3):
+        factor = lax.dot_general(
+            factors, pick[d], (((0,), (0,)), ((), ())), precision=highest, preferred_element_type=jnp.float32
+        )
+        moved = spectrum if d == 0 else pltpu.roll(spectrum, columns - 2 * d, 1)
+        for q in range(2):
+            term = factor * moved[q * spec : (q + 1) * spec]
+            totals[q] = term if totals[q] is None else totals[q] + term
+    for q in range(2):
+        hi, lo = split(totals[q])
+        gh[q * spec : (q + 1) * spec, nyq_cols] = hi
+        gl[q * spec : (q + 1) * spec, nyq_cols] = lo
+
+    back = column_pass(1, 6)
+    nyq_back = [split(back[:rows_total]), split(back[rows_total:])]
+
+    def a_copy(j):
+        return pltpu.make_async_remote_copy(
+            src_ref=afull.at[j, :, other, :],
+            dst_ref=apeer.at[j],
+            send_sem=a_send.at[j],
+            recv_sem=a_recv.at[j],
+            device_id=peer_id,
+            device_id_type=MESH,
+        )
+
+    for j in range(3):
+        for k in range(2):
+            b = 2 * j + k
+            back = column_pass(1, b)
+            parts = [split(back[:rows_total]), split(back[rows_total:])]
+            hi = jnp.concatenate([parts[0][0], parts[1][0]], axis=1)
+            lo = jnp.concatenate([parts[0][1], parts[1][1]], axis=1)
+            res = mm(hi, tx[1, 0]) + mm(hi, tx[1, 1]) + mm(lo, tx[1, 0])
+            signs = spread[:, b * columns : (b + 1) * columns]
+            for q in range(2):
+                extra = mm(nyq_back[q][0], signs) + mm(nyq_back[q][1], signs)
+                afull[j, 2 * k + q] = res[:, q * columns : (q + 1) * columns] + extra
+        a_copy(j).start()
+
+    def contribution(p, j):
+        total = None
+        for q in range(4):
+            term = apeer[j, q] * coef[g, 4 * p + q]
+            total = term if total is None else total + term
+        return total
+
+    def rs_copy(d, j, way):
+        src, dst, ssem, rsem, where = (
+            (xsend, xrecv, x_ssem, x_rsem, side_id),
+            (upsend, uprecv, up_ssem, up_rsem, up_id),
+            (dnsend, dnrecv, dn_ssem, dn_rsem, dn_id),
+        )[way]
+        return pltpu.make_async_remote_copy(
+            src_ref=src.at[d, j],
+            dst_ref=dst.at[d, j],
+            send_sem=ssem.at[d, j],
+            recv_sem=rsem.at[d, j],
+            device_id=where,
+            device_id_type=MESH,
+        )
+
+    def side_send(d, j):
+        xsend[d, j] = contribution(2 * d + 1 - xi, j)
+        rs_copy(d, j, 0).start()
+
+    for j in range(3):
+        a_copy(j).wait_recv()
+        for q in range(4):
+            apeer[j, q] = apeer[j, q] + afull[j, q, own, :]
+        when(o + line - 1 < line, lambda: side_send(o + line - 1, j))
+        when(o - line + 1 >= 0, lambda: side_send(o - line + 1, j))
+    for h in range(line - 2, -1, -1):
+        for j in range(3):
+            if h == 0:
+                side_send(o, j)
+            else:
+                when(o + h < line, lambda: side_send(o + h, j))
+                when(o - h >= 0, lambda: side_send(o - h, j))
+
+    strength_copy(0).wait_recv()
+    for way, cond in ((1, has_before), (2, has_after)):
+
+        @pl.when(cond)
+        def _(way=way):
+            strength_copy(way).wait_recv()
+
+        @pl.when(jnp.logical_not(cond))
+        def _(way=way):
+            near_strength[way - 1] = jnp.zeros(near_strength.shape[1:], jnp.float32)
+
+    full = strength[...]
+    inverse = jnp.where(full > 0, 1.0 / jnp.where(full > 0, full, 1.0), 0.0)
+    present = jnp.where(full > 0, 1.0, 0.0)
+    row_id = lax.broadcasted_iota(jnp.int32, full.shape, 0)
+    col_id = lax.broadcasted_iota(jnp.int32, full.shape, 1)
+
+    def plane_near(v):
+        total = jnp.where(row_id > 0, pltpu.roll(v, 1, 0), 0.0)
+        total = total + jnp.where(row_id < rows_total - 1, pltpu.roll(v, rows_total - 1, 0), 0.0)
+        total = total + jnp.where(col_id > 0, pltpu.roll(v, 1, 1), 0.0)
+        return total + jnp.where(col_id < columns - 1, pltpu.roll(v, columns - 1, 1), 0.0)
+
+    for j in range(3):
+        exch[j] = plane_near(mom[g, j] * inverse)
+    exch[3] = plane_near(present)
+    adjacent = []
+    for way in range(2):
+        near_s = near_strength[way]
+        there = near_s > 0
+        adjacent.append(
+            (jnp.where(there, 1.0 / jnp.where(there, near_s, 1.0), 0.0), jnp.where(there, 1.0, 0.0))
+        )
+    count = exch[3, own, :] + adjacent[0][1] + adjacent[1][1]
+    mask = jnp.where(region[0] > 0, exchange_stiffness, 0.0)
+    lower = jnp.maximum(g - 1, 0)
+    upper = jnp.minimum(g + 1, planes - 1)
+    for j in range(3):
+        near = exch[j, own, :] + mom[lower, j, own, :] * adjacent[0][0]
+        near = near + mom[upper, j, own, :] * adjacent[1][0]
+        out[j, 0] = mask * (near - count * direction[j, 0])
+
+    for h in range(line - 1, 0, -1):
+        for j in range(3):
+
+            def hop(d, way, cond):
+                stage, arrived = ((upsend, uprecv), (dnsend, dnrecv))[way - 1]
+                rs_copy(d, j, 0).wait_recv()
+                stage[d, j] = contribution(2 * d + xi, j) + xrecv[d, j]
+
+                @pl.when(cond)
+                def _():
+                    rs_copy(d, j, way).wait_recv()
+                    stage[d, j] = stage[d, j] + arrived[d, j]
+
+                rs_copy(d, j, way).start()
+
+            when(o + h < line, lambda: hop(o + h, 1, has_dn))
+            when(o - h >= 0, lambda: hop(o - h, 2, has_up))
+
+    scale = 1.0 / (4 * rows_total * columns * 2 * planes)
+    for j in range(3):
+        rs_copy(o, j, 0).wait_recv()
+        exch[j, :rows, :] = contribution(g, j) + xrecv[o, j]
+
+        @pl.when(has_dn)
+        def _():
+            rs_copy(o, j, 1).wait_recv()
+            exch[j, :rows, :] = exch[j, :rows, :] + uprecv[o, j]
+
+        @pl.when(has_up)
+        def _():
+            rs_copy(o, j, 2).wait_recv()
+            exch[j, :rows, :] = exch[j, :rows, :] + dnrecv[o, j]
+
+        out[j, 0] = out[j, 0] + exch[j, :rows, :] * scale
+
+    strength_copy(0).wait_send()
+    when(has_after, lambda: strength_copy(1).wait_send())
+    when(has_before, lambda: strength_copy(2).wait_send())
+    for j in range(3):
+        a_copy(j).wait_send()
+        for p in range(planes):
+            chunk_copy(p, j, 3).wait_send()
+        for d in range(line):
+            chunk_copy(2 * d + xi, j, 2).wait_send()
+            rs_copy(d, j, 0).wait_send()
+
+            @pl.when(jnp.logical_and(has_up, o >= d))
+            def _():
+                chunk_copy(2 * d + xi, j, 0).wait_send()
+
+            @pl.when(jnp.logical_and(has_dn, o <= d))
+            def _():
+                chunk_copy(2 * d + xi, j, 1).wait_send()
+
+            when(o < d, lambda: rs_copy(d, j, 1).wait_send())
+            when(o > d, lambda: rs_copy(d, j, 2).wait_send())
+
+
+def fused_local(direction, region, saturation, kernel_main, kernel_nyq):
+    rows, columns = direction.shape[2:]
+    planes = lax.axis_size("gz")
+    groups_y = lax.axis_size("gy")
+    rows_total = rows * groups_y
+    spec = kernel_main.shape[2]
+    line = planes // 2
+    tx, ty, gather, spread, pick, coef = (
+        jnp.asarray(t) for t in tables(columns, rows_total, groups_y, planes)
+    )
+    f32, bf16 = jnp.float32, jnp.bfloat16
+    vmem = pl.BlockSpec(memory_space=pltpu.VMEM)
+    smem = pl.BlockSpec(memory_space=pltpu.SMEM)
+    hbm = pl.BlockSpec(memory_space=pl.ANY)
+    dma = pltpu.SemaphoreType.DMA
+    stage = pltpu.VMEM((line, 3, rows, columns), f32)
+    return pl.pallas_call(
+        fused,
+        out_shape=jax.ShapeDtypeStruct(direction.shape, f32),
+        in_specs=[smem, smem, vmem, vmem, vmem, vmem, hbm, hbm, hbm, hbm, hbm],
+        out_specs=vmem,
+        scratch_shapes=[
+            pltpu.VMEM((planes, 3, rows_total, columns), f32),
+            pltpu.VMEM((rows_total, columns), f32),
+            pltpu.VMEM((2, rows, columns), f32),
+            pltpu.VMEM((4, rows_total, columns), f32),
+            pltpu.VMEM(kernel_main.shape, f32),
+            pltpu.VMEM(tx.shape, bf16),
+            pltpu.VMEM(ty.shape[1:], bf16),
+            pltpu.VMEM(gather.shape, bf16),
+            pltpu.VMEM(spread.shape, bf16),
+            pltpu.VMEM((6 * rows_total, 2 * columns), bf16),
+            pltpu.VMEM((6 * rows_total, 2 * columns), bf16),
+            pltpu.VMEM((2 * rows_total, 7 * columns), bf16),
+            pltpu.VMEM((2 * rows_total, 7 * columns), bf16),
+            pltpu.VMEM((2 * spec, 7 * columns), bf16),
+            pltpu.VMEM((2 * spec, 7 * columns), bf16),
+            pltpu.VMEM((3, 4, rows_total, columns), f32),
+            pltpu.VMEM((3, 4, rows, columns), f32),
+            stage,
+            stage,
+            stage,
+            stage,
+            stage,
+            stage,
+            dma((5,)),
+            dma((4, planes, 3)),
+            dma((planes, 3)),
+            dma((planes, 3)),
+            dma((3,)),
+            dma((3,)),
+            dma((3,)),
+            dma((3,)),
+            dma((line, 3)),
+            dma((line, 3)),
+            dma((line, 3)),
+            dma((line, 3)),
+            dma((line, 3)),
+            dma((line, 3)),
+        ],
+        compiler_params=pltpu.CompilerParams(
+            collective_id=0, has_side_effects=True, vmem_limit_bytes=40 * 1024 * 1024
+        ),
+        name="field_kernel",
+    )(coef, saturation, direction, region, pick, kernel_nyq, kernel_main, tx, ty, gather, spread)
+
+
 def solution(mesh):
     placed = (
         P(None, ("parts", "gz"), "gy", None),
@@ -190,8 +765,9 @@
         P(None, "gz", "gy", None),
         P(None, "gz", "gy"),
     )
+    small = mesh.shape["gz"] <= most_unrolled_planes and mesh.shape["gy"] == 2
     return jax.shard_map(
-        local,
+        fused_local if small else local,
         mesh=mesh,
         in_specs=placed,
         out_specs=P(None, ("parts", "gz"), "gy", None),

time: 178 us -> 51.8 us (0.29)
  waiting for transfers between devices: 81 us -> 0 us
  Pallas kernels: 0 us -> 40.9 us
  starting transfers between devices: 40.5 us -> 0 us
  matrix products: 15.2 us -> 0 us
  between operations: 14.8 us -> 0.02 us
  local copies, waits for them, and re-layouts: 18.3 us -> 10.3 us
  other arithmetic: 5.07 us -> 0 us
  blocking collectives: 2.08 us -> 0 us
    all_to_all x8 -> x0, waiting for transfers between devices: 53.1 us -> none  [the longest x1 15.7 us: local(): lax.all_to_all(done_main, 'gz', split_axis=2, concat_axis=3, tiled=True)]
    pallas_call x0 -> x1, Pallas kernels: none -> 40.9 us  [fused_local(): pl.pallas_call(fused, out_shape=jax.ShapeDtypeStruct(direction.shape, f32...]
    all_to_all x8 -> x0, starting transfers between devices: 31.7 us -> none  [the longest x1 7.15 us: local(): lax.all_to_all(spec_nyq[:, :, None], 'gz', split_axis=3, concat_axis=2, t...]
    unnamed x4 -> x0, waiting for transfers between devices: 27.9 us -> none
    dot_general x33 -> x0, matrix products: 15.2 us -> none  [the longest x4 1.35 us: plane_transform(): jnp.einsum('pz,cz...->cp...', cosine, imag_part, precision=highest)]
    ppermute x4 -> x0, starting transfers between devices: 8.7 us -> none  [the longest x2 5.94 us: with_halo(): lax.ppermute(tail, axis, [(i, (i + 1) % count) for i in range(ends)])]
    another operation x7 -> x0, local copies, waits for them, and re-layouts: 5.29 us -> none  [the longest x4 2.66 us: plane_transform(): return jnp.stack([new_real, new_imag], axis=1)]
    unnamed x25 -> x23, local copies, waits for them, and re-layouts: 6.98 us -> 10.3 us
  transfers between devices with their start and end apart: 14 -> 0, of which waited for: 9 -> 0; matrix products, arithmetic and copies ran while one was open for 15% -> 0% of each run, Pallas kernels for 0% -> 0%
where the time goes in v1:
time: 51.8 us; the launch traced here: 51.2 us
  Pallas kernels  40.9 us (79%)
  local copies, waits for them, and re-layouts  10.3 us (20%)
    pallas_call x1, Pallas kernels, fused_local(): pl.pallas_call(fused, out_shape=jax.ShapeDtypeStruct(direction.shape, f32...  40.9 us
    unnamed x23, local copies, waits for them, and re-layouts  10.3 us

profile of v1, /device:TPU:0, one launch (start us, length us, event | category | flops | bytes accessed | tf_op | source)
XLA Modules:
  0.0 51.2 jit_solution(14144109278648712085)
XLA Ops:
  0.0 0.0 copy-start.9
  0.0 0.7 %copy-done.9 = f32[8,32]{1,0:T(8,128)S(1)} copy-done((f32[8,32]{1,0:T(8,128)S(1)}, f32[8,32]{1,0:T(8,128)}, u32[]{:S(2)}) %copy-start.9) | copy-done | bytes 1048
  0.7 0.0 copy-start
  0.7 1.2 %copy-done = bf16[2,2,2,256,256]{4,3,2,1,0:T(8,128)(2,1)S(1)} copy-done((bf16[2,2,2,256,256]{4,3,2,1,0:T(8,128)(2,1)S(1)}, bf16[2,2,2,256,256]{4,3,2,1,0:T(8,128)(2,1)}, u32[]{:S(2)}) %copy-start) | copy-done | bytes 1048600
  1.9 0.0 copy-start.1
  1.9 1.1 %copy-done.1 = f32[6,2,128,128]{3,2,1,0:T(8,128)S(1)} copy-done((f32[6,2,128,128]{3,2,1,0:T(8,128)S(1)}, f32[6,2,128,128]{3,2,1,0:T(8,128)}, u32[]{:S(2)}) %copy-start.1) | copy-done | bytes 786456
  3.0 0.0 copy-start.2
  3.0 1.0 %copy-done.2 = bf16[2,2,256,256]{3,2,1,0:T(8,128)(2,1)S(1)} copy-done((bf16[2,2,256,256]{3,2,1,0:T(8,128)(2,1)S(1)}, bf16[2,2,256,256]{3,2,1,0:T(8,128)(2,1)}, u32[]{:S(2)}) %copy-start.2) | copy-done | bytes 524312
  4.1 0.0 copy-start.3
  4.1 0.9 %copy-done.3 = bf16[128,768]{1,0:T(8,128)(2,1)S(1)} copy-done((bf16[128,768]{1,0:T(8,128)(2,1)S(1)}, bf16[128,768]{1,0:T(8,128)(2,1)}, u32[]{:S(2)}) %copy-start.3) | copy-done | bytes 196632
  5.0 0.0 copy-start.4
  5.0 0.9 %copy-done.4 = bf16[768,128]{1,0:T(8,128)(2,1)S(1)} copy-done((bf16[768,128]{1,0:T(8,128)(2,1)S(1)}, bf16[768,128]{1,0:T(8,128)(2,1)}, u32[]{:S(2)}) %copy-start.4) | copy-done | bytes 196632
  5.9 0.0 copy-start.5
  5.9 0.9 %copy-done.5 = f32[3,1,64,128]{3,2,1,0:T(8,128)S(1)} copy-done((f32[3,1,64,128]{3,2,1,0:T(8,128)S(1)}, f32[3,1,64,128]{3,2,1,0:T(8,128)}, u32[]{:S(2)}) %copy-start.5) | copy-done | bytes 98328
  6.8 0.0 copy-start.6
  6.8 0.8 %copy-done.6 = s32[1,64,128]{2,1,0:T(8,128)S(1)} copy-done((s32[1,64,128]{2,1,0:T(8,128)S(1)}, s32[1,64,128]{2,1,0:T(8,128)}, u32[]{:S(2)}) %copy-start.6) | copy-done | bytes 32792
  7.6 0.0 copy-start.7
  7.6 0.7 %copy-done.7 = f32[3,12,128]{2,1,0:T(8,128)S(1)} copy-done((f32[3,12,128]{2,1,0:T(8,128)S(1)}, f32[3,12,128]{2,1,0:T(8,128)}, u32[]{:S(2)}) %copy-start.7) | copy-done | bytes 18456
  8.3 0.0 copy-start.8
  8.3 0.7 %copy-done.8 = f32[6,2,128]{2,1,0:T(2,128)S(1)} copy-done((f32[6,2,128]{2,1,0:T(2,128)S(1)}, f32[6,2,128]{2,1,0:T(2,128)}, u32[]{:S(2)}) %copy-start.8) | copy-done | bytes 6168
  9.0 0.0 copy-start.10
  9.0 0.7 %copy-done.10 = f32[3]{0:T(128)S(1)} copy-done((f32[3]{0:T(128)S(1)}, f32[3]{0:T(128)}, u32[]{:S(2)}) %copy-start.10) | copy-done | bytes 36
  9.7 40.9 %field_kernel.1 = f32[3,1,64,128]{3,2,1,0:T(8,128)S(1)} custom-call(f32[8,32]{1,0:T(8,128)S(1)} %copy-done.9, f32[3]{0:T(128)S(1)} %copy-done.10, f32[3,1,64,128]{3,2,1,0:T(8,128)S(1)} %copy-done.5, s32[1,64,128]{2,1,0:T(8,128)S(1)} %copy-done.6, f32[3,12,128]{2,1,0:T(8,128)S(1)} %copy-done.7, f32[6,2,128]{2,1,0:T(2,128)S(1)} %copy-done.8, ...), custom_call_target="tpu_custom_call" | custom-call | tf_op jit(solution)/shard_map/field_kernel/pallas_call | solution.py:709
  50.6 0.6 %copy.13 = f32[3,1,64,128]{3,2,1,0:T(8,128)} copy(f32[3,1,64,128]{3,2,1,0:T(8,128)S(1)} %field_kernel.1) | data formatting | bytes 196608
Async XLA Ops:
  0.0 0.7 %copy-start.9 = (f32[8,32]{1,0:T(8,128)S(1)}, f32[8,32]{1,0:T(8,128)}, u32[]{:S(2)}) copy-start(f32[8,32]{1,0:T(8,128)} %constant.17.clone.coef) | copy-start | bytes 3076
  0.7 1.2 %copy-start = (bf16[2,2,2,256,256]{4,3,2,1,0:T(8,128)(2,1)S(1)}, bf16[2,2,2,256,256]{4,3,2,1,0:T(8,128)(2,1)}, u32[]{:S(2)}) copy-start(bf16[2,2,2,256,256]{4,3,2,1,0:T(8,128)(2,1)} %constant.13.clone.ty_hbm) | copy-start | bytes 3145732
  1.9 1.1 %copy-start.1 = (f32[6,2,128,128]{3,2,1,0:T(8,128)S(1)}, f32[6,2,128,128]{3,2,1,0:T(8,128)}, u32[]{:S(2)}) copy-start(f32[6,2,128,128]{3,2,1,0:T(8,128)} %kmain_hbm.1) | copy-start | bytes 2359300
  3.0 1.0 %copy-start.2 = (bf16[2,2,256,256]{3,2,1,0:T(8,128)(2,1)S(1)}, bf16[2,2,256,256]{3,2,1,0:T(8,128)(2,1)}, u32[]{:S(2)}) copy-start(bf16[2,2,256,256]{3,2,1,0:T(8,128)(2,1)} %constant.12.clone.tx_hbm) | copy-start | bytes 1572868
  4.1 0.9 %copy-start.3 = (bf16[128,768]{1,0:T(8,128)(2,1)S(1)}, bf16[128,768]{1,0:T(8,128)(2,1)}, u32[]{:S(2)}) copy-start(bf16[128,768]{1,0:T(8,128)(2,1)} %constant.15.clone.spread_hbm) | copy-start | bytes 589828
  5.0 0.9 %copy-start.4 = (bf16[768,128]{1,0:T(8,128)(2,1)S(1)}, bf16[768,128]{1,0:T(8,128)(2,1)}, u32[]{:S(2)}) copy-start(bf16[768,128]{1,0:T(8,128)(2,1)} %constant.14.clone.gather_hbm) | copy-start | bytes 589828
  5.9 0.9 %copy-start.5 = (f32[3,1,64,128]{3,2,1,0:T(8,128)S(1)}, f32[3,1,64,128]{3,2,1,0:T(8,128)}, u32[]{:S(2)}) copy-start(f32[3,1,64,128]{3,2,1,0:T(8,128)} %direction.1) | copy-start | bytes 294916
  6.8 0.8 %copy-start.6 = (s32[1,64,128]{2,1,0:T(8,128)S(1)}, s32[1,64,128]{2,1,0:T(8,128)}, u32[]{:S(2)}) copy-start(s32[1,64,128]{2,1,0:T(8,128)} %region.1) | copy-start | bytes 98308
  7.6 0.7 %copy-start.7 = (f32[3,12,128]{2,1,0:T(8,128)S(1)}, f32[3,12,128]{2,1,0:T(8,128)}, u32[]{:S(2)}) copy-start(f32[3,12,128]{2,1,0:T(8,128)} %constant.16.clone.pick) | copy-start | bytes 55300
  8.3 0.7 %copy-start.8 = (f32[6,2,128]{2,1,0:T(2,128)S(1)}, f32[6,2,128]{2,1,0:T(2,128)}, u32[]{:S(2)}) copy-start(f32[6,2,128]{2,1,0:T(2,128)} %knyq.1) | copy-start | bytes 18436
  9.0 0.7 %copy-start.10 = (f32[3]{0:T(128)S(1)}, f32[3]{0:T(128)}, u32[]{:S(2)}) copy-start(f32[3]{0:T(128)} %sat.1) | copy-start | bytes 40

commit v2 on v1

--- a/solution.py
+++ b/solution.py
@@ -258,16 +258,20 @@
 def fused(
     coef,
     sat,
-    direction,
-    region,
-    pick,
-    knyq,
+    direction_hbm,
+    region_hbm,
+    pick_hbm,
+    knyq_hbm,
     kmain_hbm,
     tx_hbm,
     ty_hbm,
     gather_hbm,
     spread_hbm,
     out,
+    direction,
+    region,
+    pick,
+    knyq,
     mom,
     strength,
     near_strength,
@@ -338,13 +342,23 @@
         def _(where=where):
             pl.semaphore_signal(barrier, inc=1, device_id=where, device_id_type=MESH)
 
+    first = [
+        pltpu.make_async_copy(direction_hbm, direction, local_sem.at[5]),
+        pltpu.make_async_copy(region_hbm, region, local_sem.at[6]),
+    ]
+    for copy in first:
+        copy.start()
     loads = [
         pltpu.make_async_copy(kmain_hbm, kmain, local_sem.at[0]),
         pltpu.make_async_copy(tx_hbm, tx, local_sem.at[1]),
         pltpu.make_async_copy(ty_hbm.at[c], ty, local_sem.at[2]),
         pltpu.make_async_copy(gather_hbm, gather, local_sem.at[3]),
         pltpu.make_async_copy(spread_hbm, spread, local_sem.at[4]),
+        pltpu.make_async_copy(pick_hbm, pick, local_sem.at[7]),
+        pltpu.make_async_copy(knyq_hbm, knyq, local_sem.at[8]),
     ]
+    for copy in first:
+        copy.wait()
     for copy in loads:
         copy.start()
 
@@ -703,15 +717,19 @@
     f32, bf16 = jnp.float32, jnp.bfloat16
     vmem = pl.BlockSpec(memory_space=pltpu.VMEM)
     smem = pl.BlockSpec(memory_space=pltpu.SMEM)
-    hbm = pl.BlockSpec(memory_space=pl.ANY)
+    hbm = pl.BlockSpec(memory_space=pltpu.HBM)
     dma = pltpu.SemaphoreType.DMA
     stage = pltpu.VMEM((line, 3, rows, columns), f32)
     return pl.pallas_call(
         fused,
         out_shape=jax.ShapeDtypeStruct(direction.shape, f32),
-        in_specs=[smem, smem, vmem, vmem, vmem, vmem, hbm, hbm, hbm, hbm, hbm],
+        in_specs=[smem, smem, hbm, hbm, hbm, hbm, hbm, hbm, hbm, hbm, hbm],
         out_specs=vmem,
         scratch_shapes=[
+            pltpu.VMEM(direction.shape, f32),
+            pltpu.VMEM(region.shape, jnp.int32),
+            pltpu.VMEM(pick.shape, f32),
+            pltpu.VMEM(kernel_nyq.shape, f32),
             pltpu.VMEM((planes, 3, rows_total, columns), f32),
             pltpu.VMEM((rows_total, columns), f32),
             pltpu.VMEM((2, rows, columns), f32),
@@ -735,7 +753,7 @@
             stage,
             stage,
             stage,
-            dma((5,)),
+            dma((9,)),
             dma((4, planes, 3)),
             dma((planes, 3)),
             dma((planes, 3)),
@@ -751,7 +769,7 @@
             dma((line, 3)),
         ],
         compiler_params=pltpu.CompilerParams(
-            collective_id=0, has_side_effects=True, vmem_limit_bytes=40 * 1024 * 1024
+            collective_id=0, has_side_effects=True, vmem_limit_bytes=67043328
         ),
         name="field_kernel",
     )(coef, saturation, direction, region, pick, kernel_nyq, kernel_main, tx, ty, gather, spread)

time: 51.8 us -> 43.4 us (0.84)
  local copies, waits for them, and re-layouts: 10.3 us -> 1.54 us
  Pallas kernels: 40.9 us -> 41.7 us
    unnamed x23 -> x1, local copies, waits for them, and re-layouts: 10.3 us -> 1.54 us
    pallas_call x1, Pallas kernels: 40.9 us -> 41.7 us  [fused_local(): pl.pallas_call(fused, out_shape=jax.ShapeDtypeStruct(direction.shape, f32...]
where the time goes in v2:
time: 43.4 us; the launch traced here: 43.2 us
  Pallas kernels  41.7 us (96%)
  local copies, waits for them, and re-layouts  1.54 us (4%)
    pallas_call x1, Pallas kernels, fused_local(): pl.pallas_call(fused, out_shape=jax.ShapeDtypeStruct(direction.shape, f32...  41.7 us
    unnamed x1, local copies, waits for them, and re-layouts  1.54 us

profile of v2, /device:TPU:0, one launch (start us, length us, event | category | flops | bytes accessed | tf_op | source)
XLA Modules:
  0.0 43.2 jit_solution(9929864802570943792)
XLA Ops:
  0.0 41.7 %field_kernel.1 = f32[3,1,64,128]{3,2,1,0:T(8,128)} custom-call(f32[8,32]{1,0:T(8,128)} %constant.17.clone.coef, f32[3]{0:T(128)} %sat.1, f32[3,1,64,128]{3,2,1,0:T(8,128)} %direction_hbm.1, s32[1,64,128]{2,1,0:T(8,128)} %region_hbm.1, f32[3,12,128]{2,1,0:T(8,128)} %constant.16.clone.pick_hbm, f32[6,2,128]{2,1,0:T(2,128)} %knyq_hbm.1, ...), custom_call_target="tpu_custom_call" | custom-call | tf_op jit(solution)/shard_map/field_kernel/pallas_call | solution.py:723
  41.7 1.5 %copy.13 = f32[3,1,64,128]{3,2,1,0:T(8,128)} copy(f32[3,1,64,128]{3,2,1,0:T(8,128)} %field_kernel.1) | data formatting | bytes 196608

commit v3 on v2

--- a/solution.py
+++ b/solution.py
@@ -299,6 +299,7 @@
     ag_send,
     ag_ici,
     ag_d2d,
+    ag_psend,
     s_send,
     s_recv,
     a_send,
@@ -376,24 +377,35 @@
     pl.semaphore_wait(barrier, friends)
 
     def chunk_copy(p, j, way):
-        where, recv = ((up_id, ag_ici), (dn_id, ag_ici), (side_id, ag_ici), (peer_id, ag_d2d))[way]
+        where = (up_id, dn_id, side_id)[way]
         block = mom.at[p, j, own, :]
         return pltpu.make_async_remote_copy(
             src_ref=block,
             dst_ref=block,
             send_sem=ag_send.at[way, p, j],
-            recv_sem=recv.at[p, j],
+            recv_sem=ag_ici.at[p, j],
             device_id=where,
             device_id_type=MESH,
         )
 
-    def peer_arrival(p, j):
-        block = mom.at[p, j, other, :]
+    def peer_all(half):
+        block = mom.at[:, :, half, :]
         return pltpu.make_async_remote_copy(
             src_ref=block,
             dst_ref=block,
-            send_sem=ag_send.at[3, p, j],
-            recv_sem=ag_d2d.at[p, j],
+            send_sem=ag_psend.at[0],
+            recv_sem=ag_d2d.at[0],
+            device_id=peer_id,
+            device_id_type=MESH,
+        )
+
+    def peer_copy(p, j):
+        block = mom.at[p, j, own, :]
+        return pltpu.make_async_remote_copy(
+            src_ref=block,
+            dst_ref=block,
+            send_sem=ag_psend.at[0],
+            recv_sem=ag_d2d.at[0],
             device_id=peer_id,
             device_id_type=MESH,
         )
@@ -421,11 +433,8 @@
             device_id_type=MESH,
         )
 
-    strength_copy(0).start()
-    when(has_after, lambda: strength_copy(1).start())
-    when(has_before, lambda: strength_copy(2).start())
     for j in range(3):
-        chunk_copy(g, j, 3).start()
+        peer_copy(g, j).start()
 
     for h in range(1, line + 1):
         for j in range(3):
@@ -437,7 +446,7 @@
                     chunk_copy(p, j, 2).wait_recv()
                     when(has_up, lambda: chunk_copy(p, j, 0).start())
                     chunk_copy(p, j, 2).start()
-                    chunk_copy(p, j, 3).start()
+                    peer_copy(p, j).start()
 
                 @pl.when(o + h < line)
                 def _():
@@ -445,11 +454,11 @@
                     chunk_copy(p, j, 2).wait_recv()
                     when(has_dn, lambda: chunk_copy(p, j, 1).start())
                     chunk_copy(p, j, 2).start()
-                    chunk_copy(p, j, 3).start()
+                    peer_copy(p, j).start()
 
             def side_arrived(p):
                 chunk_copy(p, j, 2).wait_recv()
-                chunk_copy(p, j, 3).start()
+                peer_copy(p, j).start()
 
             if h == 1:
                 side_arrived(side)
@@ -457,11 +466,12 @@
                 when(o >= h - 1, lambda: side_arrived(side - 2 * (h - 1)))
                 when(o + h - 1 < line, lambda: side_arrived(side + 2 * (h - 1)))
 
+    strength_copy(0).start()
+    when(has_after, lambda: strength_copy(1).start())
+    when(has_before, lambda: strength_copy(2).start())
     for copy in loads:
         copy.wait()
-    for p in range(planes):
-        for j in range(3):
-            peer_arrival(p, j).wait_recv()
+    peer_all(other).wait_recv()
 
     step = 32
     for j in range(3):
@@ -604,47 +614,48 @@
                 when(o + h < line, lambda: side_send(o + h, j))
                 when(o - h >= 0, lambda: side_send(o - h, j))
 
-    strength_copy(0).wait_recv()
-    for way, cond in ((1, has_before), (2, has_after)):
-
-        @pl.when(cond)
-        def _(way=way):
-            strength_copy(way).wait_recv()
-
-        @pl.when(jnp.logical_not(cond))
-        def _(way=way):
-            near_strength[way - 1] = jnp.zeros(near_strength.shape[1:], jnp.float32)
-
-    full = strength[...]
-    inverse = jnp.where(full > 0, 1.0 / jnp.where(full > 0, full, 1.0), 0.0)
-    present = jnp.where(full > 0, 1.0, 0.0)
-    row_id = lax.broadcasted_iota(jnp.int32, full.shape, 0)
-    col_id = lax.broadcasted_iota(jnp.int32, full.shape, 1)
-
-    def plane_near(v):
-        total = jnp.where(row_id > 0, pltpu.roll(v, 1, 0), 0.0)
-        total = total + jnp.where(row_id < rows_total - 1, pltpu.roll(v, rows_total - 1, 0), 0.0)
-        total = total + jnp.where(col_id > 0, pltpu.roll(v, 1, 1), 0.0)
-        return total + jnp.where(col_id < columns - 1, pltpu.roll(v, columns - 1, 1), 0.0)
-
-    for j in range(3):
-        exch[j] = plane_near(mom[g, j] * inverse)
-    exch[3] = plane_near(present)
-    adjacent = []
-    for way in range(2):
-        near_s = near_strength[way]
-        there = near_s > 0
-        adjacent.append(
-            (jnp.where(there, 1.0 / jnp.where(there, near_s, 1.0), 0.0), jnp.where(there, 1.0, 0.0))
-        )
-    count = exch[3, own, :] + adjacent[0][1] + adjacent[1][1]
-    mask = jnp.where(region[0] > 0, exchange_stiffness, 0.0)
-    lower = jnp.maximum(g - 1, 0)
-    upper = jnp.minimum(g + 1, planes - 1)
-    for j in range(3):
-        near = exch[j, own, :] + mom[lower, j, own, :] * adjacent[0][0]
-        near = near + mom[upper, j, own, :] * adjacent[1][0]
-        out[j, 0] = mask * (near - count * direction[j, 0])
+    def exchange():
+        strength_copy(0).wait_recv()
+        for way, cond in ((1, has_before), (2, has_after)):
+
+            @pl.when(cond)
+            def _(way=way):
+                strength_copy(way).wait_recv()
+
+            @pl.when(jnp.logical_not(cond))
+            def _(way=way):
+                near_strength[way - 1] = jnp.zeros(near_strength.shape[1:], jnp.float32)
+
+        full = strength[...]
+        inverse = jnp.where(full > 0, 1.0 / jnp.where(full > 0, full, 1.0), 0.0)
+        present = jnp.where(full > 0, 1.0, 0.0)
+        row_id = lax.broadcasted_iota(jnp.int32, full.shape, 0)
+        col_id = lax.broadcasted_iota(jnp.int32, full.shape, 1)
+
+        def plane_near(v):
+            total = jnp.where(row_id > 0, pltpu.roll(v, 1, 0), 0.0)
+            total = total + jnp.where(row_id < rows_total - 1, pltpu.roll(v, rows_total - 1, 0), 0.0)
+            total = total + jnp.where(col_id > 0, pltpu.roll(v, 1, 1), 0.0)
+            return total + jnp.where(col_id < columns - 1, pltpu.roll(v, columns - 1, 1), 0.0)
+
+        for j in range(3):
+            exch[j] = plane_near(mom[g, j] * inverse)
+        exch[3] = plane_near(present)
+        adjacent = []
+        for way in range(2):
+            near_s = near_strength[way]
+            there = near_s > 0
+            adjacent.append(
+                (jnp.where(there, 1.0 / jnp.where(there, near_s, 1.0), 0.0), jnp.where(there, 1.0, 0.0))
+            )
+        count = exch[3, own, :] + adjacent[0][1] + adjacent[1][1]
+        mask = jnp.where(region[0] > 0, exchange_stiffness, 0.0)
+        lower = jnp.maximum(g - 1, 0)
+        upper = jnp.minimum(g + 1, planes - 1)
+        for j in range(3):
+            near = exch[j, own, :] + mom[lower, j, own, :] * adjacent[0][0]
+            near = near + mom[upper, j, own, :] * adjacent[1][0]
+            out[j, 0] = mask * (near - count * direction[j, 0])
 
     for h in range(line - 1, 0, -1):
         for j in range(3):
@@ -663,6 +674,8 @@
 
             when(o + h < line, lambda: hop(o + h, 1, has_dn))
             when(o - h >= 0, lambda: hop(o - h, 2, has_up))
+        if h == line - 1:
+            exchange()
 
     scale = 1.0 / (4 * rows_total * columns * 2 * planes)
     for j in range(3):
@@ -681,13 +694,12 @@
 
         out[j, 0] = out[j, 0] + exch[j, :rows, :] * scale
 
+    peer_all(own).wait_send()
     strength_copy(0).wait_send()
     when(has_after, lambda: strength_copy(1).wait_send())
     when(has_before, lambda: strength_copy(2).wait_send())
     for j in range(3):
         a_copy(j).wait_send()
-        for p in range(planes):
-            chunk_copy(p, j, 3).wait_send()
         for d in range(line):
             chunk_copy(2 * d + xi, j, 2).wait_send()
             rs_copy(d, j, 0).wait_send()
@@ -754,9 +766,10 @@
             stage,
             stage,
             dma((9,)),
-            dma((4, planes, 3)),
+            dma((3, planes, 3)),
             dma((planes, 3)),
-            dma((planes, 3)),
+            dma((1,)),
+            dma((1,)),
             dma((3,)),
             dma((3,)),
             dma((3,)),

time: 43.4 us -> 41.7 us (0.961)
  Pallas kernels: 41.7 us -> 40 us
    pallas_call x1, Pallas kernels: 41.7 us -> 40 us  [fused_local(): pl.pallas_call(fused, out_shape=jax.ShapeDtypeStruct(direction.shape, f32...]
where the time goes in v3:
time: 41.7 us; the launch traced here: 41.5 us
  Pallas kernels  40 us (96%)
  local copies, waits for them, and re-layouts  1.54 us (4%)
    pallas_call x1, Pallas kernels, fused_local(): pl.pallas_call(fused, out_shape=jax.ShapeDtypeStruct(direction.shape, f32...  40 us
    unnamed x1, local copies, waits for them, and re-layouts  1.54 us

profile of v3, /device:TPU:0, one launch (start us, length us, event | category | flops | bytes accessed | tf_op | source)
XLA Modules:
  0.0 41.5 jit_solution(5778858102227799751)
XLA Ops:
  0.0 40.0 %field_kernel.1 = f32[3,1,64,128]{3,2,1,0:T(8,128)} custom-call(f32[8,32]{1,0:T(8,128)} %constant.17.clone.coef, f32[3]{0:T(128)} %sat.1, f32[3,1,64,128]{3,2,1,0:T(8,128)} %direction_hbm.1, s32[1,64,128]{2,1,0:T(8,128)} %region_hbm.1, f32[3,12,128]{2,1,0:T(8,128)} %constant.16.clone.pick_hbm, f32[6,2,128]{2,1,0:T(2,128)} %knyq_hbm.1, ...), custom_call_target="tpu_custom_call" | custom-call | tf_op jit(solution)/shard_map/field_kernel/pallas_call | solution.py:735
  40.0 1.5 %copy.13 = f32[3,1,64,128]{3,2,1,0:T(8,128)} copy(f32[3,1,64,128]{3,2,1,0:T(8,128)} %field_kernel.1) | data formatting | bytes 196608
